TPU v7x, 32 devices: a whole 2x2x4 slice. The times are simulated.
32 devices in a mesh: lon: 16 (over z, x, core), lat: 2 (over y).
Axes of the slice: x: 2, y: 2, z: 4, core: 2. Of those that a mesh axis runs over, the one named last changes fastest.
Arguments:
- fields: float32 [128, 64, 4, 768], P('lat', 'lon'), may hold values from -24 to 24
- norm_gains: float32 [4, 768], replicated, may hold values from 0.25 to 1.75
- qkv_weight: bfloat16 [3, 768, 2304], replicated, may hold values from -0.21875 to 0.21875
- out_weight: bfloat16 [3, 768, 768], replicated, may hold values from -0.21875 to 0.21875
- longitude_bias: float32 [12, 64], replicated, may hold values from -3 to 380
- latitude_bias: float32 [12, 255], replicated, may hold values from -3 to 380
- level_bias: float32 [12, 7], replicated, may hold values from -3 to 380
- mlp_in: bfloat16 [768, 3072], replicated, may hold values from -0.21875 to 0.21875
- mlp_out: bfloat16 [3072, 768], replicated, may hold values from -0.109375 to 0.109375
Outputs:
- block_out: float32 [128, 64, 4, 768], P('lat', 'lon')
All inputs are finite; a program needn't handle non-finite values.
Results may differ from a plain program's by a relative error of at most 0.013.
Values may be sent and summed in bfloat16 or wider, within the bound.
A program may use at most 192 MiB of HBM per device.

v0:
```python
import functools

import jax
import jax.numpy as jnp
from jax import lax
from jax.experimental import pallas as pl
from jax.experimental.pallas import tpu as pltpu
from jax.sharding import PartitionSpec as P

HEAD = 64
EPSILON = 1e-06
LANES = 128
BLOCK = 256
NEGATIVE = -1e30
BF16 = jnp.bfloat16
F32 = jnp.float32


def normalize(fields, gain_row):
    square = jnp.mean(fields * fields, axis=-1, keepdims=True)
    return (fields * lax.rsqrt(square + EPSILON) * gain_row).astype(BF16)


def gelu(u):
    inner = u * (0.7978845608028654 + (0.7978845608028654 * 0.044715) * (u * u))
    half = 0.5 * u
    return half + half * jnp.tanh(inner)


def sweep_block(state, gain_row, qkv_ref, out_ref, bias_ref, index, group):
    tokens, features = state.shape
    normed = normalize(state, gain_row)
    qkv = jnp.dot(normed, qkv_ref[index], preferred_element_type=F32).astype(BF16)
    lane = lax.broadcasted_iota(jnp.int32, (group, LANES), 1)
    low = lane < HEAD
    scale = HEAD**-0.5
    ones = jnp.ones((group, LANES), BF16)
    columns = []
    for pair in range(features // LANES):
        rows = []
        for start in range(0, tokens, group):
            here = slice(start, start + group)
            q = qkv[here, pair * LANES : (pair + 1) * LANES]
            k = qkv[here, features + pair * LANES : features + (pair + 1) * LANES]
            v = qkv[here, 2 * features + pair * LANES : 2 * features + (pair + 1) * LANES]
            q = q * jnp.asarray(scale, BF16)
            zero = jnp.zeros_like(q)
            both = jnp.concatenate([jnp.where(low, q, zero), jnp.where(low, zero, q)], axis=0)
            scores = lax.dot_general(
                both, k, (((1,), (1,)), ((), ())), preferred_element_type=F32
            )
            scores = scores + bias_ref[2 * pair : 2 * pair + 2].reshape(2 * group, group)
            peak = jnp.max(scores, axis=-1, keepdims=True)
            weights = jnp.exp(scores - peak).astype(BF16)
            summed = jnp.dot(
                weights, jnp.concatenate([v, ones], axis=1), preferred_element_type=F32
            )
            mixed = jnp.where(low, summed[:group, :LANES], summed[group:, :LANES])
            total = jnp.where(low, summed[:group, LANES:], summed[group:, LANES:])
            rows.append((mixed / total).astype(BF16))
        columns.append(jnp.concatenate(rows, axis=0))
    attended = jnp.concatenate(columns, axis=1)
    return state + jnp.dot(attended, out_ref[index], preferred_element_type=F32)


def feed_forward(state, gain_row, in_ref, out_ref):
    features = state.shape[1]
    hidden_count = in_ref.shape[1]
    normed = normalize(state, gain_row)
    result = state
    for start in range(0, hidden_count, features):
        u = jnp.dot(normed, in_ref[:, start : start + features], preferred_element_type=F32)
        hidden = gelu(u).astype(BF16)
        result = result + jnp.dot(
            hidden, out_ref[start : start + features, :], preferred_element_type=F32
        )
    return result


def strided_rows(ref, start, count, stride):
    return jnp.concatenate(
        [ref[c, pl.ds(start, count, stride=stride), :] for c in range(ref.shape[0])], axis=1
    )


def folded_rows(ref, row, lev, count):
    return jnp.concatenate(
        [
            ref[c, pl.ds(row + half * lev, count, stride=2 * lev), :]
            for half in range(2)
            for c in range(ref.shape[0])
        ],
        axis=1,
    )


def store_strided(ref, start, count, stride, value):
    for c in range(ref.shape[0]):
        ref[c, pl.ds(start, count, stride=stride), :] = value[:, c * LANES : (c + 1) * LANES]


def fill_bias(table_ref, sweep, shift, bias_ref, length, group):
    heads = bias_ref.shape[0]
    width = table_ref.shape[2]
    rows = lax.broadcasted_iota(jnp.int32, (group, group), 0) // length
    cols = lax.broadcasted_iota(jnp.int32, (group, group), 1) // length
    for head in range(heads):
        line = jnp.broadcast_to(table_ref[sweep, head : head + 1, :], (group, width))
        line = pltpu.roll(line, shift % width, 1)
        rolled = pltpu.roll(line, 0, 1, stride=1, stride_axis=0)[:, :group]
        if length < group:
            rolled = jnp.where(rows == cols, rolled, NEGATIVE)
        bias_ref[head] = rolled


def kernel(
    sizes,
    x_ref, gains_ref, lon_ref, lat_ref, lev_ref, qkv_hbm, out_hbm, in_hbm, mlp_hbm,
    o_ref,
    qkv_ref, out_ref, in_ref, mlp_ref,
    table_ref, bias_lon, bias_lat, bias_lev,
    circ, outbox, mer, lane_row, lane_mer, lane_lev, last,
    weight_sem, send_a, recv_a, send_b, recv_b, send_c, recv_c,
):
    nlon, nlat, lev, lons, lats, rows, heads = sizes
    devices = lons * lats
    me_lon, me_lat = lax.axis_index("lon"), lax.axis_index("lat")
    me = me_lon * lats + me_lat
    local_lat = nlat // lats
    per_dest = nlon // devices
    own = local_lat * lev
    group_lon, group_lat = max(LANES, nlon), max(LANES, nlat)

    loads = []
    for s in range(3):
        loads.append(pltpu.make_async_copy(qkv_hbm.at[s], qkv_ref.at[s], weight_sem.at[2 * s]))
        loads.append(pltpu.make_async_copy(out_hbm.at[s], out_ref.at[s], weight_sem.at[2 * s + 1]))
    loads.append(pltpu.make_async_copy(in_hbm, in_ref, weight_sem.at[6]))
    loads.append(pltpu.make_async_copy(mlp_hbm, mlp_ref, weight_sem.at[7]))
    loads[0].start()
    loads[1].start()

    barrier = pltpu.get_barrier_semaphore()

    @pl.loop(1, devices)
    def _(i):
        other = lax.rem(me + i, devices)
        pl.semaphore_signal(
            barrier, inc=1,
            device_id={"lon": other // lats, "lat": lax.rem(other, lats)},
            device_id_type=pl.DeviceIdType.MESH,
        )

    pl.semaphore_wait(barrier, devices - 1)

    @pl.loop(0, rows)
    def _(r):
        pltpu.make_async_copy(
            x_ref.at[me_lon * rows + r], circ.at[r, me_lon], recv_a.at[r]
        ).start()

        @pl.loop(1, lons)
        def _(i):
            other = lax.rem(me_lon + i, lons)
            pltpu.make_async_remote_copy(
                src_ref=x_ref.at[other * rows + r],
                dst_ref=circ.at[r, me_lon],
                send_sem=send_a,
                recv_sem=recv_a.at[r],
                device_id={"lon": other, "lat": me_lat},
                device_id_type=pl.DeviceIdType.MESH,
            ).start()

    for load in loads[2:]:
        load.start()

    table_ref[...] = jnp.zeros_like(table_ref)
    for start in range(0, table_ref.shape[2], nlon):
        table_ref[0, :, start : start + nlon] = lon_ref[...]
    table_ref[1, :, : 2 * nlat - 1] = lat_ref[...]
    table_ref[2, :, : 2 * lev - 1] = lev_ref[...]
    fill_bias(table_ref, 0, 0, bias_lon, nlon, group_lon)
    fill_bias(table_ref, 1, 1 - nlat, bias_lat, nlat, group_lat)
    fill_bias(table_ref, 2, 1 - lev, bias_lev, lev, LANES)
    loads[0].wait()
    loads[1].wait()

    latitude = me_lat * local_lat + me_lon * rows

    def send_meridians(j, first, count):
        there = mer.at[j, pl.ds(latitude + first, count)]
        pltpu.make_async_copy(
            outbox.at[j, me, pl.ds(first, count)], there, recv_b.at[j]
        ).start()

        @pl.loop(1, devices)
        def _(i):
            other = lax.rem(me + i, devices)
            pltpu.make_async_remote_copy(
                src_ref=outbox.at[j, other, pl.ds(first, count)],
                dst_ref=there,
                send_sem=send_b,
                recv_sem=recv_b.at[j],
                device_id={"lon": other // lats, "lat": lax.rem(other, lats)},
                device_id_type=pl.DeviceIdType.MESH,
            ).start()

    row_tokens = nlon * lev
    features = gains_ref.shape[1]
    half_slabs = features // LANES // 2
    levels_each = max(1, BLOCK // nlon)

    @pl.loop(0, rows)
    def _(r):
        pltpu.make_async_copy(circ.at[r], circ.at[r], recv_a.at[r]).wait()
        arrived = circ[r].astype(F32).reshape(row_tokens, features)
        for c in range(features // LANES):
            lane_row[c] = arrived[:, c * LANES : (c + 1) * LANES]
        for first in range(0, lev, levels_each):
            levels = range(first, first + levels_each)
            state = jnp.concatenate(
                [strided_rows(lane_row, level, nlon, lev) for level in levels], axis=0
            )
            state = sweep_block(
                state, gains_ref[0:1, :], qkv_ref, out_ref, bias_lon, 0, group_lon
            )
            for at, level in enumerate(levels):
                store_strided(lane_row, level, nlon, lev, state[at * nlon : (at + 1) * nlon])
        upper = lax.broadcasted_iota(jnp.int32, (row_tokens, LANES), 0) % (2 * lev) >= lev
        for c in range(half_slabs):
            left, right = lane_row[c], lane_row[c + half_slabs]
            packed = (
                jnp.where(upper, pltpu.roll(right, lev, 0), left),
                jnp.where(upper, right, pltpu.roll(left, row_tokens - lev, 0)),
            )
            for j in range(per_dest):
                outbox[j, :, r, :, c * LANES : (c + 1) * LANES] = (
                    packed[j].reshape(devices, 2 * lev, LANES).astype(BF16)
                )

        if rows > 1:
            @pl.when(r == rows - 2)
            def _():
                send_meridians(0, 0, rows - 1)

    send_meridians(0, rows - 1, 1)
    for j in range(1, per_dest):
        send_meridians(j, 0, rows)

    for load in loads[2:]:
        load.wait()

    lat_each = BLOCK // nlat
    half_steps = per_dest * (lats - 1)

    @pl.loop(0, per_dest * lats)
    def _(t):
        j = t // lats
        turn = lax.rem(t, lats)
        target = lax.rem(me_lat + 1 + turn, lats)

        @pl.when(turn == 0)
        def _():
            pltpu.make_async_copy(mer.at[j], mer.at[j], recv_b.at[j]).wait()
            for c in range(half_slabs):
                lane_mer[c] = (
                    mer[j, :, :, c * LANES : (c + 1) * LANES]
                    .astype(F32)
                    .reshape(nlat * 2 * lev, LANES)
                )

            @pl.loop(0, lev // lat_each)
            def _(b):
                state = jnp.concatenate(
                    [
                        folded_rows(lane_mer, b * lat_each + a, lev, nlat)
                        for a in range(lat_each)
                    ],
                    axis=0,
                )
                state = sweep_block(
                    state, gains_ref[1:2, :], qkv_ref, out_ref, bias_lat, 1, group_lat
                )
                for a in range(lat_each):
                    store_strided(
                        lane_lev, b * lat_each + a, nlat, lev,
                        state[a * nlat : (a + 1) * nlat],
                    )

        start = pl.multiple_of(target * own, own)
        for piece in range(0, own, BLOCK):
            state = jnp.concatenate(
                [
                    lane_lev[c, pl.ds(start + piece, BLOCK), :]
                    for c in range(features // LANES)
                ],
                axis=1,
            )
            state = sweep_block(state, gains_ref[2:3, :], qkv_ref, out_ref, bias_lev, 2, LANES)
            state = feed_forward(state, gains_ref[3:4, :], in_ref, mlp_ref)
            last[t, piece : piece + BLOCK, :] = state.astype(BF16)

        @pl.when(turn < lats - 1)
        def _():
            pltpu.make_async_remote_copy(
                src_ref=last.at[t],
                dst_ref=o_ref.at[me_lat * per_dest + j],
                send_sem=send_c,
                recv_sem=recv_c,
                device_id={"lon": me_lon, "lat": target},
                device_id_type=pl.DeviceIdType.MESH,
            ).start()

        @pl.when(turn == lats - 1)
        def _():
            pltpu.make_async_copy(
                last.at[t], o_ref.at[me_lat * per_dest + j], recv_c
            ).start()

    pltpu.make_async_copy(o_ref, o_ref, recv_c).wait()
    if half_steps:
        sent = last.at[pl.ds(0, half_steps)]
        pltpu.make_async_copy(sent, sent, send_c).wait()

    @pl.loop(0, rows)
    def _(r):
        if lons > 1:
            sent = circ.at[r, pl.ds(0, lons - 1)]
            pltpu.make_async_copy(sent, sent, send_a).wait()

    for j in range(per_dest):
        sent = outbox.at[j, pl.ds(0, devices - 1)]
        pltpu.make_async_copy(sent, sent, send_b).wait()


def per_device(
    lons, lats,
    fields, norm_gains, qkv_weight, out_weight,
    longitude_bias, latitude_bias, level_bias, mlp_in, mlp_out,
):
    local_lat, local_lon, lev, features = fields.shape
    nlon, nlat = local_lon * lons, local_lat * lats
    rows = local_lat // lons
    devices = lons * lats
    per_dest = nlon // devices
    heads = longitude_bias.shape[0]
    hidden = mlp_in.shape[1]
    slabs = features // LANES
    width = max(2 * LANES, 2 * nlat, nlon)
    x = fields.astype(BF16).reshape(local_lat, local_lon * lev, features)
    group_lon, group_lat = max(LANES, nlon), max(LANES, nlat)
    vmem = pl.BlockSpec(memory_space=pltpu.VMEM)
    hbm = pl.BlockSpec(memory_space=pl.ANY)
    own = local_lat * lev
    out = pl.pallas_call(
        functools.partial(kernel, (nlon, nlat, lev, lons, lats, rows, heads)),
        out_shape=jax.ShapeDtypeStruct((local_lon, own, features), BF16),
        in_specs=[hbm, vmem, vmem, vmem, vmem, hbm, hbm, hbm, hbm],
        out_specs=hbm,
        scratch_shapes=[
            pltpu.VMEM(qkv_weight.shape, BF16),
            pltpu.VMEM(out_weight.shape, BF16),
            pltpu.VMEM(mlp_in.shape, BF16),
            pltpu.VMEM(mlp_out.shape, BF16),
            pltpu.VMEM((3, heads, width), F32),
            pltpu.VMEM((heads, group_lon, group_lon), F32),
            pltpu.VMEM((heads, group_lat, group_lat), F32),
            pltpu.VMEM((heads, LANES, LANES), F32),
            pltpu.VMEM((rows, lons, local_lon * lev, features), BF16),
            pltpu.VMEM((per_dest, devices, rows, 2 * lev, features // 2), BF16),
            pltpu.VMEM((per_dest, nlat, 2 * lev, features // 2), BF16),
            pltpu.VMEM((slabs, nlon * lev, LANES), F32),
            pltpu.VMEM((slabs // 2, nlat * 2 * lev, LANES), F32),
            pltpu.VMEM((slabs, nlat * lev, LANES), F32),
            pltpu.VMEM((per_dest * lats, own, features), BF16),
            pltpu.SemaphoreType.DMA((8,)),
            pltpu.SemaphoreType.DMA,
            pltpu.SemaphoreType.DMA((rows,)),
            pltpu.SemaphoreType.DMA,
            pltpu.SemaphoreType.DMA((per_dest,)),
            pltpu.SemaphoreType.DMA,
            pltpu.SemaphoreType.DMA,
        ],
        compiler_params=pltpu.CompilerParams(
            collective_id=0, has_side_effects=True, vmem_limit_bytes=64 * 1000 * 1000
        ),
    )(x, norm_gains, longitude_bias, latitude_bias, level_bias, qkv_weight, out_weight, mlp_in, mlp_out)
    out = out.reshape(local_lon, local_lat, lev, features)
    return jnp.swapaxes(out, 0, 1).astype(fields.dtype)


def solution(mesh):
    in_specs = (P("lat", "lon", None, None), P(), P(), P(), P(), P(), P(), P(), P())
    out_specs = P("lat", "lon", None, None)
    return jax.shard_map(
        functools.partial(per_device, mesh.shape["lon"], mesh.shape["lat"]),
        mesh=mesh, in_specs=in_specs, out_specs=out_specs, check_vma=False,
    )
```

profile of v0, /device:TPU:11, one launch (start us, length us, event | category | flops | bytes accessed | tf_op | source)
XLA Modules:
  0.0 119.1 jit_solution(15235604423684135430)
XLA Ops:
  0.0 1.4 %copy.10.lev_ref = f32[12,7]{1,0:T(8,128)} copy(f32[12,7]{0,1:T(8,128)} %param.15) | data formatting | bytes 672 | tf_op args[6]
  1.4 2.5 %convert_element_type.12 = bf16[64,4,4,768]{3,2,1,0:T(4,128)(2,1)S(1)} convert(f32[64,4,4,768]{3,2,1,0:T(4,128)} %param.9) | non-fusion elementwise | flops 786432 | bytes 4718592 | tf_op jit(solution)/shard_map/convert_element_type | solution.py:350
  3.8 1.3 %reshape.6.x_ref = bf16[64,16,768]{2,1,0:T(8,128)(2,1)} reshape(bf16[64,4,4,768]{3,2,1,0:T(4,128)(2,1)S(1)} %convert_element_type.12) | data formatting | bytes 3145728 | tf_op jit(solution)/shard_map/reshape | solution.py:350
  5.2 108.3 %shard_map.91 = bf16[4,256,768]{2,1,0:T(8,128)(2,1)} custom-call(bf16[64,16,768]{2,1,0:T(8,128)(2,1)} %reshape.6.x_ref, f32[4,768]{1,0:T(4,128)} %gains_ref.1, f32[12,64]{1,0:T(8,128)} %lon_ref.1, f32[12,255]{1,0:T(8,128)} %lat_ref.1, f32[12,7]{1,0:T(8,128)} %copy.10.lev_ref, bf16[3,768,2304]{2,1,0:T(8,128)(2,1)} %qkv_hbm.1, bf16[3,768,768]{2,1,0:T(8,128)(2,1)} %out_hbm.1, ...), custom_call_target="tpu_custom_call" | custom-call | tf_op jit(solution)/shard_map/pallas_call | solution.py:355
  113.5 2.9 %reshape.7 = f32[4,64,4,768]{3,2,1,0:T(4,128)S(1)} reshape(bf16[4,256,768]{2,1,0:T(8,128)(2,1)} %shard_map.91) | data formatting | bytes 4718592 | tf_op jit(solution)/shard_map/convert_element_type | solution.py:389
  116.4 2.6 %copy.13 = f32[4,64,4,768]{3,2,0,1:T(4,128)} copy(f32[4,64,4,768]{3,2,1,0:T(4,128)S(1)} %reshape.7) | data formatting | bytes 6291456 | tf_op jit(solution)/shard_map/convert_element_type | solution.py:389
where the time goes:
time: 121 us; the launch traced here: 119 us
  Pallas kernels  108 us (89%)
  local copies, waits for them, and re-layouts  8.23 us (7%)
  other arithmetic  2.47 us (2%)
    pallas_call x1, Pallas kernels, per_device(): pl.pallas_call(functools.partial(kernel, (nlon, nlat, lev, lons, lats, ro...  108 us
    convert_element_type x2, local copies, waits for them, and re-layouts, per_device(): return jnp.swapaxes(out, 0, 1).astype(fields.dtype)  5.53 us
    convert_element_type x1, other arithmetic, per_device(): x = fields.astype(BF16).reshape(local_lat, local_lon * lev, features)  2.47 us

commit v1 on v0

--- a/solution.py
+++ b/solution.py
@@ -31,33 +31,40 @@
     tokens, features = state.shape
     normed = normalize(state, gain_row)
     qkv = jnp.dot(normed, qkv_ref[index], preferred_element_type=F32).astype(BF16)
-    lane = lax.broadcasted_iota(jnp.int32, (group, LANES), 1)
-    low = lane < HEAD
-    scale = HEAD**-0.5
-    ones = jnp.ones((group, LANES), BF16)
+    low = lax.broadcasted_iota(jnp.int32, (group, LANES), 1) < HEAD
+    zero = jnp.zeros((group, LANES), BF16)
+    one = jnp.ones((group, LANES), BF16)
+    sums = (jnp.where(low, one, zero), jnp.where(low, zero, one))
+    scale = jnp.asarray(HEAD**-0.5, BF16)
     columns = []
     for pair in range(features // LANES):
         rows = []
         for start in range(0, tokens, group):
             here = slice(start, start + group)
-            q = qkv[here, pair * LANES : (pair + 1) * LANES]
+            q = qkv[here, pair * LANES : (pair + 1) * LANES] * scale
             k = qkv[here, features + pair * LANES : features + (pair + 1) * LANES]
             v = qkv[here, 2 * features + pair * LANES : 2 * features + (pair + 1) * LANES]
-            q = q * jnp.asarray(scale, BF16)
-            zero = jnp.zeros_like(q)
-            both = jnp.concatenate([jnp.where(low, q, zero), jnp.where(low, zero, q)], axis=0)
+            keys = jnp.concatenate([jnp.where(low, k, zero), jnp.where(low, zero, k)], axis=0)
             scores = lax.dot_general(
-                both, k, (((1,), (1,)), ((), ())), preferred_element_type=F32
-            )
-            scores = scores + bias_ref[2 * pair : 2 * pair + 2].reshape(2 * group, group)
-            peak = jnp.max(scores, axis=-1, keepdims=True)
-            weights = jnp.exp(scores - peak).astype(BF16)
+                q, keys, (((1,), (1,)), ((), ())), preferred_element_type=F32
+            )
+            scores = scores + bias_ref[pair]
+            halves = []
+            for head in range(2):
+                part = scores[:, head * group : (head + 1) * group]
+                peak = jnp.max(part, axis=-1, keepdims=True)
+                halves.append(jnp.exp(part - peak).astype(BF16))
+            values = jnp.concatenate(
+                [
+                    jnp.concatenate([jnp.where(low, v, zero), sums[0]], axis=1),
+                    jnp.concatenate([jnp.where(low, zero, v), sums[1]], axis=1),
+                ],
+                axis=0,
+            )
             summed = jnp.dot(
-                weights, jnp.concatenate([v, ones], axis=1), preferred_element_type=F32
-            )
-            mixed = jnp.where(low, summed[:group, :LANES], summed[group:, :LANES])
-            total = jnp.where(low, summed[:group, LANES:], summed[group:, LANES:])
-            rows.append((mixed / total).astype(BF16))
+                jnp.concatenate(halves, axis=1), values, preferred_element_type=F32
+            )
+            rows.append((summed[:, :LANES] / summed[:, LANES:]).astype(BF16))
         columns.append(jnp.concatenate(rows, axis=0))
     attended = jnp.concatenate(columns, axis=1)
     return state + jnp.dot(attended, out_ref[index], preferred_element_type=F32)
@@ -100,7 +107,7 @@
 
 
 def fill_bias(table_ref, sweep, shift, bias_ref, length, group):
-    heads = bias_ref.shape[0]
+    heads = 2 * bias_ref.shape[0]
     width = table_ref.shape[2]
     rows = lax.broadcasted_iota(jnp.int32, (group, group), 0) // length
     cols = lax.broadcasted_iota(jnp.int32, (group, group), 1) // length
@@ -110,7 +117,7 @@
         rolled = pltpu.roll(line, 0, 1, stride=1, stride_axis=0)[:, :group]
         if length < group:
             rolled = jnp.where(rows == cols, rolled, NEGATIVE)
-        bias_ref[head] = rolled
+        bias_ref[head // 2, :, head % 2 * group : (head % 2 + 1) * group] = rolled
 
 
 def kernel(
@@ -186,11 +193,13 @@
     loads[1].wait()
 
     latitude = me_lat * local_lat + me_lon * rows
-
-    def send_meridians(j, first, count):
+    outer = (me_lon < lons // 4) | (me_lon >= lons - lons // 4)
+    outer, inner = jnp.logical_not(outer), outer
+
+    def send_meridians(j, first, count, part):
         there = mer.at[j, pl.ds(latitude + first, count)]
         pltpu.make_async_copy(
-            outbox.at[j, me, pl.ds(first, count)], there, recv_b.at[j]
+            outbox.at[j, me, pl.ds(first, count)], there, recv_b.at[j, part]
         ).start()
 
         @pl.loop(1, devices)
@@ -200,10 +209,14 @@
                 src_ref=outbox.at[j, other, pl.ds(first, count)],
                 dst_ref=there,
                 send_sem=send_b,
-                recv_sem=recv_b.at[j],
+                recv_sem=recv_b.at[j, part],
                 device_id={"lon": other // lats, "lat": lax.rem(other, lats)},
                 device_id_type=pl.DeviceIdType.MESH,
             ).start()
+
+    def wait_meridians(j, count, part):
+        arrived = mer.at[j, pl.ds(0, devices * count)]
+        pltpu.make_async_copy(arrived, arrived, recv_b.at[j, part]).wait()
 
     row_tokens = nlon * lev
     features = gains_ref.shape[1]
@@ -213,6 +226,12 @@
     @pl.loop(0, rows)
     def _(r):
         pltpu.make_async_copy(circ.at[r], circ.at[r], recv_a.at[r]).wait()
+
+        if rows > 1:
+            @pl.when(inner & (r == rows - 1))
+            def _():
+                send_meridians(0, 0, rows - 1, 0)
+
         arrived = circ[r].astype(F32).reshape(row_tokens, features)
         for c in range(features // LANES):
             lane_row[c] = arrived[:, c * LANES : (c + 1) * LANES]
@@ -239,13 +258,16 @@
                 )
 
         if rows > 1:
-            @pl.when(r == rows - 2)
+            @pl.when(outer & (r == rows - 2))
             def _():
-                send_meridians(0, 0, rows - 1)
-
-    send_meridians(0, rows - 1, 1)
-    for j in range(1, per_dest):
-        send_meridians(j, 0, rows)
+                send_meridians(0, 0, rows - 1, 0)
+
+    send_meridians(0, rows - 1, 1, 1)
+
+    @pl.when(outer)
+    def _():
+        for j in range(1, per_dest):
+            send_meridians(j, 0, rows, 0)
 
     for load in loads[2:]:
         load.wait()
@@ -261,7 +283,21 @@
 
         @pl.when(turn == 0)
         def _():
-            pltpu.make_async_copy(mer.at[j], mer.at[j], recv_b.at[j]).wait()
+            @pl.when(j == 0)
+            def _():
+                if rows > 1:
+                    wait_meridians(j, rows - 1, 0)
+                wait_meridians(j, 1, 1)
+
+            if per_dest > 1:
+                @pl.when(j > 0)
+                def _():
+                    wait_meridians(j, rows, 0)
+
+                @pl.when(inner & (j < per_dest - 1))
+                def _():
+                    send_meridians(j + 1, 0, rows, 0)
+
             for c in range(half_slabs):
                 lane_mer[c] = (
                     mer[j, :, :, c * LANES : (c + 1) * LANES]
@@ -363,9 +399,9 @@
             pltpu.VMEM(mlp_in.shape, BF16),
             pltpu.VMEM(mlp_out.shape, BF16),
             pltpu.VMEM((3, heads, width), F32),
-            pltpu.VMEM((heads, group_lon, group_lon), F32),
-            pltpu.VMEM((heads, group_lat, group_lat), F32),
-            pltpu.VMEM((heads, LANES, LANES), F32),
+            pltpu.VMEM((heads // 2, group_lon, 2 * group_lon), F32),
+            pltpu.VMEM((heads // 2, group_lat, 2 * group_lat), F32),
+            pltpu.VMEM((heads // 2, LANES, 2 * LANES), F32),
             pltpu.VMEM((rows, lons, local_lon * lev, features), BF16),
             pltpu.VMEM((per_dest, devices, rows, 2 * lev, features // 2), BF16),
             pltpu.VMEM((per_dest, nlat, 2 * lev, features // 2), BF16),
@@ -377,7 +413,7 @@
             pltpu.SemaphoreType.DMA,
             pltpu.SemaphoreType.DMA((rows,)),
             pltpu.SemaphoreType.DMA,
-            pltpu.SemaphoreType.DMA((per_dest,)),
+            pltpu.SemaphoreType.DMA((per_dest, 2)),
             pltpu.SemaphoreType.DMA,
             pltpu.SemaphoreType.DMA,
         ],

time: 121 us -> 108 us (0.89)
  Pallas kernels: 108 us -> 96.2 us
    pallas_call x1, Pallas kernels: 108 us -> 96.2 us  [per_device(): pl.pallas_call(functools.partial(kernel, (nlon, nlat, lev, lons, lats, ro...]
where the time goes in v1:
time: 108 us; the launch traced here: 107 us
  Pallas kernels  96.2 us (89%)
  local copies, waits for them, and re-layouts  8.23 us (8%)
  other arithmetic  2.47 us (2%)
    pallas_call x1, Pallas kernels, per_device(): pl.pallas_call(functools.partial(kernel, (nlon, nlat, lev, lons, lats, ro...  96.2 us
    convert_element_type x2, local copies, waits for them, and re-layouts, per_device(): return jnp.swapaxes(out, 0, 1).astype(fields.dtype)  5.53 us
    convert_element_type x1, other arithmetic, per_device(): x = fields.astype(BF16).reshape(local_lat, local_lon * lev, features)  2.47 us

profile of v1, /device:TPU:11, one launch (start us, length us, event | category | flops | bytes accessed | tf_op | source)
XLA Modules:
  0.0 106.9 jit_solution(17855742366585221088)
XLA Ops:
  0.0 1.4 %copy.10.lev_ref = f32[12,7]{1,0:T(8,128)} copy(f32[12,7]{0,1:T(8,128)} %param.15) | data formatting | bytes 672 | tf_op args[6]
  1.4 2.5 %convert_element_type.12 = bf16[64,4,4,768]{3,2,1,0:T(4,128)(2,1)S(1)} convert(f32[64,4,4,768]{3,2,1,0:T(4,128)} %param.9) | non-fusion elementwise | flops 786432 | bytes 4718592 | tf_op jit(solution)/shard_map/convert_element_type | solution.py:386
  3.8 1.3 %reshape.6.x_ref = bf16[64,16,768]{2,1,0:T(8,128)(2,1)} reshape(bf16[64,4,4,768]{3,2,1,0:T(4,128)(2,1)S(1)} %convert_element_type.12) | data formatting | bytes 3145728 | tf_op jit(solution)/shard_map/reshape | solution.py:386
  5.2 96.2 %shard_map.91 = bf16[4,256,768]{2,1,0:T(8,128)(2,1)} custom-call(bf16[64,16,768]{2,1,0:T(8,128)(2,1)} %reshape.6.x_ref, f32[4,768]{1,0:T(4,128)} %gains_ref.1, f32[12,64]{1,0:T(8,128)} %lon_ref.1, f32[12,255]{1,0:T(8,128)} %lat_ref.1, f32[12,7]{1,0:T(8,128)} %copy.10.lev_ref, bf16[3,768,2304]{2,1,0:T(8,128)(2,1)} %qkv_hbm.1, bf16[3,768,768]{2,1,0:T(8,128)(2,1)} %out_hbm.1, ...), custom_call_target="tpu_custom_call" | custom-call | tf_op jit(solution)/shard_map/pallas_call | solution.py:391
  101.4 2.9 %reshape.7 = f32[4,64,4,768]{3,2,1,0:T(4,128)S(1)} reshape(bf16[4,256,768]{2,1,0:T(8,128)(2,1)} %shard_map.91) | data formatting | bytes 4718592 | tf_op jit(solution)/shard_map/convert_element_type | solution.py:425
  104.3 2.6 %copy.13 = f32[4,64,4,768]{3,2,0,1:T(4,128)} copy(f32[4,64,4,768]{3,2,1,0:T(4,128)S(1)} %reshape.7) | data formatting | bytes 6291456 | tf_op jit(solution)/shard_map/convert_element_type | solution.py:425

commit v2 on v1

--- a/solution.py
+++ b/solution.py
@@ -185,7 +185,10 @@
     for start in range(0, table_ref.shape[2], nlon):
         table_ref[0, :, start : start + nlon] = lon_ref[...]
     table_ref[1, :, : 2 * nlat - 1] = lat_ref[...]
-    table_ref[2, :, : 2 * lev - 1] = lev_ref[...]
+    square = bias_lev.at[0, :, :LANES]
+    square[...] = jnp.zeros(square.shape, F32)
+    square[: 2 * lev - 1, :heads] = lev_ref[...]
+    table_ref[2, :, : 2 * lev - 1] = square[...].T[:heads, : 2 * lev - 1]
     fill_bias(table_ref, 0, 0, bias_lon, nlon, group_lon)
     fill_bias(table_ref, 1, 1 - nlat, bias_lat, nlat, group_lat)
     fill_bias(table_ref, 2, 1 - lev, bias_lev, lev, LANES)
@@ -334,13 +337,15 @@
             )
             state = sweep_block(state, gains_ref[2:3, :], qkv_ref, out_ref, bias_lev, 2, LANES)
             state = feed_forward(state, gains_ref[3:4, :], in_ref, mlp_ref)
-            last[t, piece : piece + BLOCK, :] = state.astype(BF16)
+            last[t, piece // lev : (piece + BLOCK) // lev] = (
+                state.reshape(BLOCK // lev, lev, features).astype(BF16)
+            )
 
         @pl.when(turn < lats - 1)
         def _():
             pltpu.make_async_remote_copy(
                 src_ref=last.at[t],
-                dst_ref=o_ref.at[me_lat * per_dest + j],
+                dst_ref=o_ref.at[:, me_lat * per_dest + j],
                 send_sem=send_c,
                 recv_sem=recv_c,
                 device_id={"lon": me_lon, "lat": target},
@@ -350,7 +355,7 @@
         @pl.when(turn == lats - 1)
         def _():
             pltpu.make_async_copy(
-                last.at[t], o_ref.at[me_lat * per_dest + j], recv_c
+                last.at[t], o_ref.at[:, me_lat * per_dest + j], recv_c
             ).start()
 
     pltpu.make_async_copy(o_ref, o_ref, recv_c).wait()
@@ -383,14 +388,13 @@
     hidden = mlp_in.shape[1]
     slabs = features // LANES
     width = max(2 * LANES, 2 * nlat, nlon)
-    x = fields.astype(BF16).reshape(local_lat, local_lon * lev, features)
+    x = fields.astype(BF16)
     group_lon, group_lat = max(LANES, nlon), max(LANES, nlat)
     vmem = pl.BlockSpec(memory_space=pltpu.VMEM)
     hbm = pl.BlockSpec(memory_space=pl.ANY)
-    own = local_lat * lev
     out = pl.pallas_call(
         functools.partial(kernel, (nlon, nlat, lev, lons, lats, rows, heads)),
-        out_shape=jax.ShapeDtypeStruct((local_lon, own, features), BF16),
+        out_shape=jax.ShapeDtypeStruct((local_lat, local_lon, lev, features), BF16),
         in_specs=[hbm, vmem, vmem, vmem, vmem, hbm, hbm, hbm, hbm],
         out_specs=hbm,
         scratch_shapes=[
@@ -402,13 +406,13 @@
             pltpu.VMEM((heads // 2, group_lon, 2 * group_lon), F32),
             pltpu.VMEM((heads // 2, group_lat, 2 * group_lat), F32),
             pltpu.VMEM((heads // 2, LANES, 2 * LANES), F32),
-            pltpu.VMEM((rows, lons, local_lon * lev, features), BF16),
+            pltpu.VMEM((rows, lons, local_lon, lev, features), BF16),
             pltpu.VMEM((per_dest, devices, rows, 2 * lev, features // 2), BF16),
             pltpu.VMEM((per_dest, nlat, 2 * lev, features // 2), BF16),
             pltpu.VMEM((slabs, nlon * lev, LANES), F32),
             pltpu.VMEM((slabs // 2, nlat * 2 * lev, LANES), F32),
             pltpu.VMEM((slabs, nlat * lev, LANES), F32),
-            pltpu.VMEM((per_dest * lats, own, features), BF16),
+            pltpu.VMEM((per_dest * lats, local_lat, lev, features), BF16),
             pltpu.SemaphoreType.DMA((8,)),
             pltpu.SemaphoreType.DMA,
             pltpu.SemaphoreType.DMA((rows,)),
@@ -420,9 +424,8 @@
         compiler_params=pltpu.CompilerParams(
             collective_id=0, has_side_effects=True, vmem_limit_bytes=64 * 1000 * 1000
         ),
-    )(x, norm_gains, longitude_bias, latitude_bias, level_bias, qkv_weight, out_weight, mlp_in, mlp_out)
-    out = out.reshape(local_lon, local_lat, lev, features)
-    return jnp.swapaxes(out, 0, 1).astype(fields.dtype)
+    )(x, norm_gains, longitude_bias, latitude_bias, level_bias.T, qkv_weight, out_weight, mlp_in, mlp_out)
+    return out.astype(fields.dtype)
 
 
 def solution(mesh):

time: 108 us -> 105 us (0.972)
  local copies, waits for them, and re-layouts: 8.23 us -> 0 us
  other arithmetic: 2.47 us -> 7.6 us
    convert_element_type x2 -> x0, local copies, waits for them, and re-layouts: 5.53 us -> none  [per_device(): return jnp.swapaxes(out, 0, 1).astype(fields.dtype)]
    convert_element_type x1 -> x2, other arithmetic: 2.47 us -> 7.6 us  [the longest x1 3.99 us: per_device(): return out.astype(fields.dtype)]
    unnamed x1 -> x0, local copies, waits for them, and re-layouts: 1.36 us -> none
    reshape x1 -> x0, local copies, waits for them, and re-layouts: 1.34 us -> none  [per_device(): x = fields.astype(BF16).reshape(local_lat, local_lon * lev, features)]
where the time goes in v2:
time: 105 us; the launch traced here: 104 us
  Pallas kernels  96.2 us (92%)
  other arithmetic  7.6 us (7%)
    pallas_call x1, Pallas kernels, per_device(): pl.pallas_call(functools.partial(kernel, (nlon, nlat, lev, lons, lats, ro...  96.2 us
    convert_element_type x1, other arithmetic, per_device(): return out.astype(fields.dtype)  3.99 us
    convert_element_type x1, other arithmetic, per_device(): x = fields.astype(BF16)  3.61 us

profile of v2, /device:TPU:11, one launch (start us, length us, event | category | flops | bytes accessed | tf_op | source)
XLA Modules:
  0.0 103.8 jit_solution(16811764244164791799)
XLA Ops:
  0.0 3.6 %convert_element_type.6.x_ref = bf16[64,4,4,768]{3,2,1,0:T(4,128)(2,1)} convert(f32[64,4,4,768]{3,2,1,0:T(4,128)} %param.9) | non-fusion elementwise | flops 786432 | bytes 4718592 | tf_op jit(solution)/shard_map/convert_element_type | solution.py:391
  3.6 96.2 %shard_map.91 = bf16[64,4,4,768]{3,2,1,0:T(4,128)(2,1)} custom-call(bf16[64,4,4,768]{3,2,1,0:T(4,128)(2,1)} %convert_element_type.6.x_ref, f32[4,768]{1,0:T(4,128)} %gains_ref.1, f32[12,64]{1,0:T(8,128)} %lon_ref.1, f32[12,255]{1,0:T(8,128)} %lat_ref.1, f32[7,12]{1,0:T(8,128)} %bitcast.1, bf16[3,768,2304]{2,1,0:T(8,128)(2,1)} %qkv_hbm.1, ...), custom_call_target="tpu_custom_call" | custom-call | tf_op jit(solution)/shard_map/pallas_call | solution.py:395
  99.8 4.0 %convert_element_type.7 = f32[64,4,4,768]{3,2,1,0:T(4,128)} convert(bf16[64,4,4,768]{3,2,1,0:T(4,128)(2,1)} %shard_map.91) | non-fusion elementwise | flops 786432 | bytes 4718592 | tf_op jit(solution)/shard_map/convert_element_type | solution.py:428

commit v3 on v2

--- a/solution.py
+++ b/solution.py
@@ -126,8 +126,8 @@
     o_ref,
     qkv_ref, out_ref, in_ref, mlp_ref,
     table_ref, bias_lon, bias_lat, bias_lev,
-    circ, outbox, mer, lane_row, lane_mer, lane_lev, last,
-    weight_sem, send_a, recv_a, send_b, recv_b, send_c, recv_c,
+    wide, narrow, circ, outbox, mer, lane_row, lane_mer, lane_lev, last,
+    fields_sem, weight_sem, send_a, recv_a, send_b, recv_b, send_c, recv_c,
 ):
     nlon, nlat, lev, lons, lats, rows, heads = sizes
     devices = lons * lats
@@ -144,8 +144,11 @@
         loads.append(pltpu.make_async_copy(out_hbm.at[s], out_ref.at[s], weight_sem.at[2 * s + 1]))
     loads.append(pltpu.make_async_copy(in_hbm, in_ref, weight_sem.at[6]))
     loads.append(pltpu.make_async_copy(mlp_hbm, mlp_ref, weight_sem.at[7]))
-    loads[0].start()
-    loads[1].start()
+    fields_in = [
+        pltpu.make_async_copy(x_ref.at[:, r], wide.at[r], fields_sem.at[r]) for r in range(rows)
+    ]
+    for load in fields_in + loads[:2]:
+        load.start()
 
     barrier = pltpu.get_barrier_semaphore()
 
@@ -162,15 +165,17 @@
 
     @pl.loop(0, rows)
     def _(r):
+        pltpu.make_async_copy(x_ref.at[:, r], wide.at[r], fields_sem.at[r]).wait()
+        narrow[r] = wide[r].astype(BF16)
         pltpu.make_async_copy(
-            x_ref.at[me_lon * rows + r], circ.at[r, me_lon], recv_a.at[r]
+            narrow.at[r, me_lon], circ.at[r, me_lon], recv_a.at[r]
         ).start()
 
         @pl.loop(1, lons)
         def _(i):
             other = lax.rem(me_lon + i, lons)
             pltpu.make_async_remote_copy(
-                src_ref=x_ref.at[other * rows + r],
+                src_ref=narrow.at[r, other],
                 dst_ref=circ.at[r, me_lon],
                 send_sem=send_a,
                 recv_sem=recv_a.at[r],
@@ -388,7 +393,7 @@
     hidden = mlp_in.shape[1]
     slabs = features // LANES
     width = max(2 * LANES, 2 * nlat, nlon)
-    x = fields.astype(BF16)
+    x = fields.reshape(lons, rows, local_lon, lev, features)
     group_lon, group_lat = max(LANES, nlon), max(LANES, nlat)
     vmem = pl.BlockSpec(memory_space=pltpu.VMEM)
     hbm = pl.BlockSpec(memory_space=pl.ANY)
@@ -406,6 +411,8 @@
             pltpu.VMEM((heads // 2, group_lon, 2 * group_lon), F32),
             pltpu.VMEM((heads // 2, group_lat, 2 * group_lat), F32),
             pltpu.VMEM((heads // 2, LANES, 2 * LANES), F32),
+            pltpu.VMEM((rows, lons, local_lon, lev, features), F32),
+            pltpu.VMEM((rows, lons, local_lon, lev, features), BF16),
             pltpu.VMEM((rows, lons, local_lon, lev, features), BF16),
             pltpu.VMEM((per_dest, devices, rows, 2 * lev, features // 2), BF16),
             pltpu.VMEM((per_dest, nlat, 2 * lev, features // 2), BF16),
@@ -413,6 +420,7 @@
             pltpu.VMEM((slabs // 2, nlat * 2 * lev, LANES), F32),
             pltpu.VMEM((slabs, nlat * lev, LANES), F32),
             pltpu.VMEM((per_dest * lats, local_lat, lev, features), BF16),
+            pltpu.SemaphoreType.DMA((rows,)),
             pltpu.SemaphoreType.DMA((8,)),
             pltpu.SemaphoreType.DMA,
             pltpu.SemaphoreType.DMA((rows,)),

time: 105 us -> 102 us (0.971)
  other arithmetic: 7.6 us -> 3.99 us
    convert_element_type x1 -> x0, other arithmetic: 3.61 us -> none  [per_device(): x = fields.astype(BF16)]
where the time goes in v3:
time: 102 us; the launch traced here: 100 us
  Pallas kernels  96.4 us (95%)
  other arithmetic  3.99 us (4%)
    pallas_call x1, Pallas kernels, per_device(): pl.pallas_call(functools.partial(kernel, (nlon, nlat, lev, lons, lats, ro...  96.4 us
    convert_element_type x1, other arithmetic, per_device(): return out.astype(fields.dtype)  3.99 us

profile of v3, /device:TPU:11, one launch (start us, length us, event | category | flops | bytes accessed | tf_op | source)
XLA Modules:
  0.0 100.4 jit_solution(16319505193562759215)
XLA Ops:
  0.0 96.4 %shard_map.91 = bf16[64,4,4,768]{3,2,1,0:T(4,128)(2,1)} custom-call(f32[16,4,4,4,768]{4,3,2,1,0:T(4,128)} %bitcast.2, f32[4,768]{1,0:T(4,128)} %gains_ref.1, f32[12,64]{1,0:T(8,128)} %lon_ref.1, f32[12,255]{1,0:T(8,128)} %lat_ref.1, f32[7,12]{1,0:T(8,128)} %bitcast.3, bf16[3,768,2304]{2,1,0:T(8,128)(2,1)} %qkv_hbm.1, bf16[3,768,768]{2,1,0:T(8,128)(2,1)} %out_hbm.1, ...), custom_call_target="tpu_custom_call" | custom-call | tf_op jit(solution)/shard_map/pallas_call | solution.py:400
  96.4 4.0 %convert_element_type.3 = f32[64,4,4,768]{3,2,1,0:T(4,128)} convert(bf16[64,4,4,768]{3,2,1,0:T(4,128)(2,1)} %shard_map.91) | non-fusion elementwise | flops 786432 | bytes 4718592 | tf_op jit(solution)/shard_map/convert_element_type | solution.py:436

commit v4 on v3

--- a/solution.py
+++ b/solution.py
@@ -295,6 +295,11 @@
             def _():
                 if rows > 1:
                     wait_meridians(j, rows - 1, 0)
+                if per_dest > 1:
+                    @pl.when(inner)
+                    def _():
+                        send_meridians(1, 0, rows, 0)
+
                 wait_meridians(j, 1, 1)
 
             if per_dest > 1:
@@ -302,7 +307,7 @@
                 def _():
                     wait_meridians(j, rows, 0)
 
-                @pl.when(inner & (j < per_dest - 1))
+                @pl.when(inner & (j > 0) & (j < per_dest - 1))
                 def _():
                     send_meridians(j + 1, 0, rows, 0)
 

time: 102 us -> 109 us (1.069); the launches traced: 100 us -> 109 us
  Pallas kernels: 96.4 us -> 105 us
    pallas_call x1, Pallas kernels: 96.4 us -> 105 us  [per_device(): pl.pallas_call(functools.partial(kernel, (nlon, nlat, lev, lons, lats, ro...]
where the time goes in v4:
time: 109 us
  Pallas kernels  105 us (96%)
  other arithmetic  3.99 us (4%)
    pallas_call x1, Pallas kernels, per_device(): pl.pallas_call(functools.partial(kernel, (nlon, nlat, lev, lons, lats, ro...  105 us
    convert_element_type x1, other arithmetic, per_device(): return out.astype(fields.dtype)  3.99 us

profile of v4, /device:TPU:11, one launch (start us, length us, event | category | flops | bytes accessed | tf_op | source)
XLA Modules:
  0.0 108.7 jit_solution(565051598409787194)
XLA Ops:
  0.0 104.7 %shard_map.91 = bf16[64,4,4,768]{3,2,1,0:T(4,128)(2,1)} custom-call(f32[16,4,4,4,768]{4,3,2,1,0:T(4,128)} %bitcast.2, f32[4,768]{1,0:T(4,128)} %gains_ref.1, f32[12,64]{1,0:T(8,128)} %lon_ref.1, f32[12,255]{1,0:T(8,128)} %lat_ref.1, f32[7,12]{1,0:T(8,128)} %bitcast.3, bf16[3,768,2304]{2,1,0:T(8,128)(2,1)} %qkv_hbm.1, bf16[3,768,768]{2,1,0:T(8,128)(2,1)} %out_hbm.1, ...), custom_call_target="tpu_custom_call" | custom-call | tf_op jit(solution)/shard_map/pallas_call | solution.py:405
  104.7 4.0 %convert_element_type.3 = f32[64,4,4,768]{3,2,1,0:T(4,128)} convert(bf16[64,4,4,768]{3,2,1,0:T(4,128)(2,1)} %shard_map.91) | non-fusion elementwise | flops 786432 | bytes 4718592 | tf_op jit(solution)/shard_map/convert_element_type | solution.py:441
